TPU v7x, 32 devices: a whole 2x2x4 slice. The times are simulated.
32 devices in a mesh: win: 8 (over z, x), fsdp: 4 (over y, core).
Axes of the slice: x: 2, y: 2, z: 4, core: 2. Of those that a mesh axis runs over, the one named last changes fastest.
Arguments:
- queries: bfloat16 [8192, 2560], P(('win', 'fsdp')), may hold values from -5 to 5
- keys: bfloat16 [8192, 2560], P(('win', 'fsdp')), may hold values from -5 to 5
- values: bfloat16 [8192, 2560], P(('win', 'fsdp')), may hold values from -6 to 6
- stream: bfloat16 [8192, 5120], P(('win', 'fsdp')), may hold values from -0.59765625 to 0.59765625
- out_weight: bfloat16 [2560, 5120], P('fsdp', 'win'), may hold values from -0.125 to 0.125
- gate: float32 [5120], replicated, may hold values from 0.5 to 2
- head_shift: float32 [5120], replicated, may hold values from -3 to 3
- head_scale: float32 [5120], replicated, may hold values from 0.25 to 1.75
- head_weight: bfloat16 [5120, 64], replicated, may hold values from -0.078125 to 0.078125
- latents: float32 [128, 4096], P('win', 'fsdp'), may hold values from -6 to 6
- step_size: float32 [1], replicated, may hold values from 0.5 to 1
- intersections: int32 [8], replicated, may hold values from 1 to 4
- ramps: int32 [8, 4, 2], replicated, may hold values from 1 to 16
Outputs:
- blended: float32 [128, 4096], P('win', 'fsdp')
All inputs are finite; a program needn't handle non-finite values.
Results may differ from a plain program's by a relative error of at most 0.0065.
Values may be sent and summed in bfloat16 or wider, within the bound.
A program may use at most 128 MiB of HBM per device.

v0:
```python
import math

import jax
import jax.numpy as jnp
from jax import lax
from jax.sharding import PartitionSpec as P

HEADS = 20
HD = 128
FD = 4


EPSILON = 0.001


def padded_2(value, sides, width):
    for axis, dim in sides:
        size, length = (lax.axis_size(axis), value.shape[dim])
        up = [(i, (i + 1) % size) for i in range(size)]
        down = [(j, i) for i, j in up]
        last = lax.slice_in_dim(value, length - width, length, axis=dim)
        initial = lax.slice_in_dim(value, 0, width, axis=dim)
        before = lax.ppermute(last, axis, up)
        after = lax.ppermute(initial, axis, down)
        value = jnp.concatenate([before, value, after], axis=dim)
    return value


def softmax_block(query_h, key_h, value_h, score_scale):
    scores = (
        jnp.einsum("qhd,khd->hqk", query_h, key_h, preferred_element_type=jnp.float32) * score_scale
    )
    highest = jnp.max(scores, axis=-1, keepdims=True)
    exponent = jnp.exp(scores - highest)
    denominator = jnp.sum(exponent, axis=-1)
    probability = exponent.astype(jnp.bfloat16)
    summed = jnp.einsum("hqk,khd->qhd", probability, value_h, preferred_element_type=jnp.float32)
    return summed / jnp.transpose(denominator)[:, :, None]


def local(
    queries,
    keys,
    values,
    stream,
    out_weight,
    gate,
    head_shift,
    head_scale,
    head_weight,
    latents,
    step_size,
    intersections,
    ramps,
):
    tok_rows, feat_width = queries.shape
    groups = lax.axis_size("fsdp")
    head_count = HEADS
    score_scale = 1.0 / math.sqrt(HD)
    per_group = head_count // groups
    split_shape = (tok_rows, groups, per_group, HD)
    query_part = lax.all_to_all(
        queries.reshape(split_shape), "fsdp", split_axis=1, concat_axis=0, tiled=True
    )
    key_part = lax.all_to_all(
        keys.reshape(split_shape), "fsdp", split_axis=1, concat_axis=0, tiled=True
    )
    value_part = lax.all_to_all(
        values.reshape(split_shape), "fsdp", split_axis=1, concat_axis=0, tiled=True
    )
    result = softmax_block(query_part[:, 0], key_part[:, 0], value_part[:, 0], score_scale)
    own_heads = result.astype(jnp.bfloat16)[:, None]
    window_rows = own_heads.shape[0]
    own_heads = own_heads.reshape(window_rows, per_group * HD)
    full_columns = lax.all_gather(out_weight, "win", axis=1, tiled=True)
    projected = lax.psum_scatter(
        jnp.dot(own_heads, full_columns, preferred_element_type=jnp.float32).astype(jnp.bfloat16),
        "fsdp",
        scatter_dimension=0,
        tiled=True,
    ).astype(jnp.float32)
    hidden = stream.astype(jnp.float32) + gate * projected
    centre = jnp.mean(hidden, axis=-1, keepdims=True)
    centred = hidden - centre
    variance = jnp.mean(centred * centred, axis=-1, keepdims=True)
    normed = centred / jnp.sqrt(variance + EPSILON)
    modulated = (normed * head_scale + head_shift).astype(jnp.bfloat16)
    velocity = jnp.dot(modulated, head_weight, preferred_element_type=jnp.float32)
    fresh = latents + step_size[0] * velocity.reshape(latents.shape)
    frames_dev = latents.shape[0]
    shared = FD
    padded = padded_2(fresh.astype(jnp.bfloat16), (("win", 0),), shared).astype(fresh.dtype)
    prev_block = padded[:shared]
    next_block = padded[shared + frames_dev :]
    window = lax.axis_index("win")
    win_count = lax.axis_size("win")
    prev_window = (window + win_count - 1) % win_count
    window_ids = jnp.arange(win_count, dtype=jnp.int32)
    over_prev = jnp.sum(jnp.where(window_ids == prev_window, intersections, 0))
    over_next = jnp.sum(jnp.where(window_ids == window, intersections, 0))
    ramp_prev = jnp.sum(
        jnp.where((window_ids == prev_window)[:, None, None], ramps, 0), axis=0
    ).astype(jnp.float32)
    ramp_own = jnp.sum(jnp.where((window_ids == window)[:, None, None], ramps, 0), axis=0).astype(
        jnp.float32
    )
    frame_ids = jnp.arange(frames_dev, dtype=jnp.int32)
    shared_ids = jnp.arange(shared, dtype=jnp.int32)
    inside_prev = frame_ids < over_prev
    select_prev = (
        (shared_ids[None, :] == shared - over_prev + frame_ids[:, None]) & inside_prev[:, None]
    ).astype(jnp.float32)
    prev_aligned = jnp.dot(select_prev, prev_block, precision=lax.Precision.HIGHEST)
    rows_prev = (shared_ids[None, :] == frame_ids[:, None]).astype(jnp.float32)
    ramp_rows_prev = jnp.dot(rows_prev, ramp_prev, precision=lax.Precision.HIGHEST)
    weight_before = ramp_rows_prev[:, 0:1]
    weight_self = ramp_rows_prev[:, 1:2]
    spare_prev = 1.0 - (frame_ids < shared).astype(jnp.float32)[:, None]
    blend_prev = (weight_before * prev_aligned + weight_self * fresh) / (
        weight_before + weight_self + spare_prev
    )
    shifted = frame_ids - (frames_dev - over_next)
    inside_next = shifted >= 0
    select_next = (shared_ids[None, :] == shifted[:, None]).astype(jnp.float32)
    next_aligned = jnp.dot(select_next, next_block, precision=lax.Precision.HIGHEST)
    ramp_rows = jnp.dot(select_next, ramp_own, precision=lax.Precision.HIGHEST)
    weight_mine = ramp_rows[:, 0:1]
    weight_after = ramp_rows[:, 1:2]
    spare = 1.0 - inside_next.astype(jnp.float32)[:, None]
    blend_next = (weight_mine * fresh + weight_after * next_aligned) / (
        weight_mine + weight_after + spare
    )
    return jnp.where(
        inside_prev[:, None], blend_prev, jnp.where(inside_next[:, None], blend_next, fresh)
    )


def solution(mesh):
    in_specs = (
        P(("win", "fsdp"), None),
        P(("win", "fsdp"), None),
        P(("win", "fsdp"), None),
        P(("win", "fsdp"), None),
        P("fsdp", "win"),
        P(),
        P(),
        P(),
        P(),
        P("win", "fsdp"),
        P(),
        P(),
        P(),
    )
    out_specs = P("win", "fsdp")
    return jax.shard_map(local, mesh=mesh, in_specs=in_specs, out_specs=out_specs, check_vma=False)
```

profile of v0, /device:TPU:0, one launch (start us, length us, event | category | flops | bytes accessed | tf_op | source)
XLA Modules:
  0.0 235.3 jit_solution(2147026987415011485)
XLA Ops:
  6.5 0.0 copy-start
  6.5 0.0 copy-start.5
  6.5 0.0 all-gather.2.cloned.1.call-start
  6.5 0.7 all-gather.2.cloned.1.call-update
  7.3 2.4 %copy.18 = bf16[256,2560]{0,1:T(8,128)(2,1)} copy(bf16[256,2560]{1,0:T(8,128)(2,1)} %param.13) | data formatting | bytes 2621440 | tf_op args[0]
  9.7 4.3 %all-to-all-start = ((bf16[256,4,5,128]{0,3,2,1:T(8,128)(2,1)}), bf16[256,4,5,128]{0,3,2,1:T(8,128)(2,1)S(1)}, u32[]{:S(2)}, u32[]{:S(2)}) async-start(bf16[256,4,5,128]{0,3,2,1:T(8,128)(2,1)} %bitcast.2), calls=%async_computation | async-start | bytes 2621440 | tf_op jit(solution)/shard_map/all_to_all | solution.py:62
  14.0 0.0 copy-done.5
  14.0 1.4 copy.20
  15.4 15.8 %all-to-all-done = bf16[256,4,5,128]{0,3,2,1:T(8,128)(2,1)S(1)} async-done(((bf16[256,4,5,128]{0,3,2,1:T(8,128)(2,1)}), bf16[256,4,5,128]{0,3,2,1:T(8,128)(2,1)S(1)}, u32[]{:S(2)}, u32[]{:S(2)}) %all-to-all-start) | async-done | bytes 1310752 | tf_op jit(solution)/shard_map/all_to_all | solution.py:62
  31.2 3.5 %all-to-all-start.1 = ((bf16[256,4,5,128]{0,3,2,1:T(8,128)(2,1)}), bf16[256,4,5,128]{0,3,2,1:T(8,128)(2,1)S(1)}, u32[]{:S(2)}, u32[]{:S(2)}) async-start(bf16[256,4,5,128]{0,3,2,1:T(8,128)(2,1)} %bitcast.49), calls=%async_computation.1 | async-start | bytes 2621440 | tf_op jit(solution)/shard_map/all_to_all | solution.py:65
  34.7 2.4 %copy.22 = bf16[256,2560]{0,1:T(8,128)(2,1)} copy(bf16[256,2560]{1,0:T(8,128)(2,1)} %param.15) | data formatting | bytes 2621440 | tf_op args[2]
  37.2 14.8 %all-to-all-done.1 = bf16[256,4,5,128]{0,3,2,1:T(8,128)(2,1)S(1)} async-done(((bf16[256,4,5,128]{0,3,2,1:T(8,128)(2,1)}), bf16[256,4,5,128]{0,3,2,1:T(8,128)(2,1)S(1)}, u32[]{:S(2)}, u32[]{:S(2)}) %all-to-all-start.1) | async-done | bytes 1310752 | tf_op jit(solution)/shard_map/all_to_all | solution.py:65
  52.0 0.0 copy-start.4
  52.0 4.3 %all-to-all-start.2 = ((bf16[256,4,5,128]{0,3,2,1:T(8,128)(2,1)}), bf16[256,4,5,128]{0,3,2,1:T(8,128)(2,1)}, u32[]{:S(2)}, u32[]{:S(2)}) async-start(bf16[256,4,5,128]{0,3,2,1:T(8,128)(2,1)} %bitcast.48), calls=%async_computation.2 | async-start | bytes 2621440 | tf_op jit(solution)/shard_map/all_to_all | solution.py:68
  56.3 0.0 reduce-scatter.2.cloned.1.call-start
  56.3 0.0 copy-done.4
  56.3 0.8 copy.19
  57.1 1.8 copy.21
  58.9 14.7 %all-to-all-done.2 = bf16[256,4,5,128]{0,3,2,1:T(8,128)(2,1)} async-done(((bf16[256,4,5,128]{0,3,2,1:T(8,128)(2,1)}), bf16[256,4,5,128]{0,3,2,1:T(8,128)(2,1)}, u32[]{:S(2)}, u32[]{:S(2)}) %all-to-all-start.2) | async-done | bytes 1310752 | tf_op jit(solution)/shard_map/all_to_all | solution.py:68
  73.6 3.4 %copy.23 = bf16[4,256,1,5,128]{1,0,4,3,2:T(4,128)(2,1)} copy(bf16[4,256,1,5,128]{1,4,3,0,2:T(8,128)(2,1)} %bitcast.12) | data formatting | bytes 2621440 | tf_op jit(solution)/shard_map/all_to_all | solution.py:68
  77.0 3.7 %squeeze.15 = bf16[1024,5,128]{0,2,1:T(8,128)(2,1)} reshape(bf16[4,256,1,5,128]{1,0,4,3,2:T(4,128)(2,1)} %copy.23) | data formatting | bytes 2621440 | tf_op jit(solution)/shard_map/squeeze | solution.py:71
  80.6 2.9 %multiply_reduce_fusion = (f32[5,1024]{1,0:T(8,128)S(1)}, f32[5,1024,1024]{1,2,0:T(8,128)S(1)}) fusion(bf16[1024,5,128]{2,0,1:T(8,128)(2,1)S(1)} %bitcast.44, bf16[1024,5,128]{2,0,1:T(8,128)(2,1)S(1)} %bitcast.45), kind=kOutput, calls=%fused_computation.1 | convolution fusion | flops 1352657920 | bytes 23613440 | tf_op jit(solution)/shard_map/qhd,khd->hqk/dot_general | solution.py:31
  83.5 0.0 copy-start.1
  83.5 0.0 copy-start.6
  83.5 3.7 %fusion = f32[5,1024]{1,0:T(8,128)S(1)} fusion(f32[5,1024,1024]{1,2,0:T(8,128)S(1)} %get-tuple-element.20, f32[5,1024]{1,0:T(8,128)S(1)} %get-tuple-element.19), kind=kLoop, calls=%fused_computation.2 | loop fusion | flops 15723520 | bytes 21012480 | tf_op jit(solution)/shard_map/reduce_sum | solution.py:35
  87.2 3.7 %copy-done.1 = f32[5,1024,1024]{1,2,0:T(8,128)} copy-done((f32[5,1024,1024]{1,2,0:T(8,128)}, f32[5,1024,1024]{1,2,0:T(8,128)S(1)}, u32[]{:S(2)}) %copy-start.1) | copy-done | bytes 20971544
  91.0 0.0 copy-done.6
  91.0 11.2 %fusion.7 = bf16[1024,5,128]{0,2,1:T(8,128)(2,1)S(1)} fusion(bf16[1024,5,128]{0,2,1:T(8,128)(2,1)S(1)} %copy-done.6, f32[5,1024,1024]{1,2,0:T(8,128)} %copy-done.1, f32[5,1024]{1,0:T(8,128)S(1)} %get-tuple-element.19, f32[1024,5]{0,1:T(8,128)S(1)} %bitcast.50), kind=kOutput, calls=%fused_computation.13 | convolution fusion | flops 1359216640 | bytes 23633920 | tf_op jit(solution)/shard_map/hqk,khd->qhd/dot_general | solution.py:37
  102.2 12.1 %all-gather.2.cloned.1.call-done = bf16[640,5120]{1,0:T(8,128)(2,1)} async-done(((bf16[640,640]{1,0:T(8,128)(2,1)}), bf16[640,5120]{1,0:T(8,128)(2,1)}) %all-gather.2.cloned.1.call-update) | async-done | bytes 6553616 | tf_op jit(solution)/shard_map/all_gather | solution.py:75
  114.3 13.8 %convolution_convert_fusion = bf16[1024,5120]{1,0:T(8,128)(2,1)} fusion(bf16[1024,640]{0,1:T(8,128)(2,1)S(1)} %bitcast.51, bf16[640,5120]{1,0:T(8,128)(2,1)} %all-gather.2.cloned.1.call-done), kind=kOutput, calls=%fused_computation.7 | convolution fusion | flops 6716129280 | bytes 18350080 | tf_op jit(solution)/shard_map/dot_general | solution.py:77
  128.1 0.0 copy-start.10
  128.1 0.0 copy-start.9
  128.1 0.0 copy-start.2
  128.1 0.0 copy-start.7
  128.1 0.0 reduce-scatter.2.cloned.1.call-update
  128.9 0.0 copy-done.10
  129.0 0.7 select_reduce_fusion.3
  130.9 0.6 iota_compare_fusion.8
  131.6 0.0 copy-done.9
  131.6 0.2 select_reduce_fusion.1
  131.8 0.2 fusion.18
  132.0 0.2 fusion.19
  132.2 0.0 copy-start.11
  132.2 0.0 copy-start.12
  132.2 78.6 %reduce-scatter.2.cloned.1.call-done = bf16[256,5120]{1,0:T(8,128)(2,1)} async-done(((bf16[1024,5120]{1,0:T(8,128)(2,1)}), bf16[256,5120]{1,0:T(8,128)(2,1)}) %reduce-scatter.2.cloned.1.call-update) | async-done | bytes 2621456 | tf_op jit(solution)/shard_map/reduce_scatter | solution.py:76
  210.9 0.0 copy-done.2
  210.9 0.0 copy-done.7
  210.9 2.8 %fusion.6 = f32[256]{0:T(256)S(1)} fusion(bf16[256,5120]{1,0:T(8,128)(2,1)} %reduce-scatter.2.cloned.1.call-done, bf16[256,5120]{1,0:T(8,128)(2,1)S(1)} %copy-done.2, f32[5120]{0:T(1024)S(1)} %copy-done.7), kind=kLoop, calls=%fused_computation.11 | loop fusion | flops 6553344 | bytes 5264384 | tf_op jit(solution)/shard_map/reduce_sum | solution.py:83
  213.7 0.0 copy-done.3
  213.7 1.3 multiply_reduce_fusion.1
  215.0 0.0 copy-done
  215.0 0.0 copy-done.11
  215.0 0.0 copy-done.12
  215.0 0.0 copy-start.8
  215.1 1.7 fusion.17
  216.7 0.1 copy.25
  216.8 0.1 mul.85
  216.9 0.0 copy-done.8
  217.0 4.3 %collective-permute-start.1 = (bf16[4,1024]{1,0:T(4,128)(2,1)S(1)}, bf16[4,1024]{1,0:T(4,128)(2,1)S(1)}, u32[]{:S(2)}, u32[]{:S(2)}) collective-permute-start(bf16[4,1024]{1,0:T(4,128)(2,1)S(1)} %get-tuple-element.12), channel_id=1, source_target_pairs={{4,0},{8,4},{12,8},{16,12},{20,16},{24,20},{28,24},{0,28},{5,1},{9... | collective-permute-start | bytes 24584 | tf_op jit(solution)/shard_map/ppermute | solution.py:24
  221.3 0.0 collective-permute-start
  221.3 1.4 collective-permute-done.1
  222.7 0.2 fusion.13
  222.9 4.8 %collective-permute-done = bf16[4,1024]{1,0:T(4,128)(2,1)S(1)} collective-permute-done((bf16[4,1024]{1,0:T(4,128)(2,1)S(1)}, bf16[4,1024]{1,0:T(4,128)(2,1)S(1)}, u32[]{:S(2)}, u32[]{:S(2)}) %collective-permute-start) | collective-permute-done | bytes 8224 | tf_op jit(solution)/shard_map/ppermute | solution.py:23
  227.6 0.8 fusion.16
  (11 shorter events, 0.1 us)
Async XLA Ops:
  6.5 208.5 %copy-start = (bf16[5120,64]{0,1:T(8,128)(2,1)S(1)}, bf16[5120,64]{0,1:T(8,128)(2,1)}, u32[]{:S(2)}) copy-start(bf16[5120,64]{0,1:T(8,128)(2,1)} %param.21) | copy-start | bytes 1966084
  6.5 7.4 %copy-start.5 = (bf16[256,2560]{1,0:T(8,128)(2,1)S(1)}, bf16[256,2560]{1,0:T(8,128)(2,1)}, u32[]{:S(2)}) copy-start(bf16[256,2560]{1,0:T(8,128)(2,1)} %param.14) | copy-start | bytes 3932164
  6.5 107.7 %all-gather.2.cloned.1.call-start = ((), (), s32[]{:S(2)}) async-start(), calls=%async_computation.4 | async-start | bytes 7372800 | tf_op jit(solution)/shard_map/all_gather | solution.py:75
  9.7 21.5 %all-to-all-start = ((bf16[256,4,5,128]{0,3,2,1:T(8,128)(2,1)}), bf16[256,4,5,128]{0,3,2,1:T(8,128)(2,1)S(1)}, u32[]{:S(2)}, u32[]{:S(2)}) async-start(bf16[256,4,5,128]{0,3,2,1:T(8,128)(2,1)} %bitcast.2), calls=%async_computation | async-start | bytes 2621440 | tf_op jit(solution)/shard_map/all_to_all | solution.py:62
  31.2 20.8 %all-to-all-start.1 = ((bf16[256,4,5,128]{0,3,2,1:T(8,128)(2,1)}), bf16[256,4,5,128]{0,3,2,1:T(8,128)(2,1)S(1)}, u32[]{:S(2)}, u32[]{:S(2)}) async-start(bf16[256,4,5,128]{0,3,2,1:T(8,128)(2,1)} %bitcast.49), calls=%async_computation.1 | async-start | bytes 2621440 | tf_op jit(solution)/shard_map/all_to_all | solution.py:65
  52.0 4.4 %copy-start.4 = (bf16[256,4,5,128]{0,3,2,1:T(8,128)(2,1)}, bf16[256,4,5,128]{0,3,2,1:T(8,128)(2,1)S(1)}, u32[]{:S(2)}) copy-start(bf16[256,4,5,128]{0,3,2,1:T(8,128)(2,1)S(1)} %all-to-all-done.1) | copy-start | bytes 3932164
  52.0 21.6 %all-to-all-start.2 = ((bf16[256,4,5,128]{0,3,2,1:T(8,128)(2,1)}), bf16[256,4,5,128]{0,3,2,1:T(8,128)(2,1)}, u32[]{:S(2)}, u32[]{:S(2)}) async-start(bf16[256,4,5,128]{0,3,2,1:T(8,128)(2,1)} %bitcast.48), calls=%async_computation.2 | async-start | bytes 2621440 | tf_op jit(solution)/shard_map/all_to_all | solution.py:68
  56.3 154.6 %reduce-scatter.2.cloned.1.call-start = ((), (), s32[]{:S(2)}) async-start(), calls=%async_computation.5 | async-start | bytes 13107200 | tf_op jit(solution)/shard_map/reduce_scatter | solution.py:76
  83.5 7.4 %copy-start.1 = (f32[5,1024,1024]{1,2,0:T(8,128)}, f32[5,1024,1024]{1,2,0:T(8,128)S(1)}, u32[]{:S(2)}) copy-start(f32[5,1024,1024]{1,2,0:T(8,128)S(1)} %get-tuple-element.20) | copy-start | bytes 62914564
  83.5 7.4 %copy-start.6 = (bf16[1024,5,128]{0,2,1:T(8,128)(2,1)S(1)}, bf16[1024,5,128]{0,2,1:T(8,128)(2,1)}, u32[]{:S(2)}) copy-start(bf16[1024,5,128]{0,2,1:T(8,128)(2,1)} %squeeze.15) | copy-start | bytes 3932164
  128.1 0.9 copy-start.10
  128.1 3.5 %copy-start.9 = (s32[8,4,2]{0,2,1:T(2,128)S(1)}, s32[8,4,2]{0,2,1:T(2,128)}, u32[]{:S(2)}) copy-start(s32[8,4,2]{0,2,1:T(2,128)} %param.25) | copy-start | bytes 772
  128.1 82.8 %copy-start.2 = (bf16[256,5120]{1,0:T(8,128)(2,1)S(1)}, bf16[256,5120]{1,0:T(8,128)(2,1)}, u32[]{:S(2)}) copy-start(bf16[256,5120]{1,0:T(8,128)(2,1)} %param.16) | copy-start | bytes 7864324
  128.1 82.8 %copy-start.7 = (f32[5120]{0:T(1024)S(1)}, f32[5120]{0:T(1024)}, u32[]{:S(2)}) copy-start(f32[5120]{0:T(1024)} %param.18) | copy-start | bytes 61444
  132.2 82.8 %copy-start.11 = (f32[5120]{0:T(1024)S(1)}, f32[5120]{0:T(1024)}, u32[]{:S(2)}) copy-start(f32[5120]{0:T(1024)} %param.19) | copy-start | bytes 61444
  132.2 82.8 %copy-start.12 = (f32[5120]{0:T(1024)S(1)}, f32[5120]{0:T(1024)}, u32[]{:S(2)}) copy-start(f32[5120]{0:T(1024)} %param.20) | copy-start | bytes 61444
  210.9 2.8 %copy-start.3 = (bf16[256,5120]{1,0:T(8,128)(2,1)S(1)}, bf16[256,5120]{1,0:T(8,128)(2,1)}, u32[]{:S(2)}) copy-start(bf16[256,5120]{1,0:T(8,128)(2,1)} %reduce-scatter.2.cloned.1.call-done) | copy-start | bytes 7864324
  215.0 1.9 copy-start.8
  217.0 5.7 %collective-permute-start.1 = (bf16[4,1024]{1,0:T(4,128)(2,1)S(1)}, bf16[4,1024]{1,0:T(4,128)(2,1)S(1)}, u32[]{:S(2)}, u32[]{:S(2)}) collective-permute-start(bf16[4,1024]{1,0:T(4,128)(2,1)S(1)} %get-tuple-element.12), channel_id=1, source_target_pairs={{4,0},{8,4},{12,8},{16,12},{20,16},{24,20},{28,24},{0,28},{5,1},{9... | collective-permute-start | bytes 24584 | tf_op jit(solution)/shard_map/ppermute | solution.py:24
  221.3 6.3 %collective-permute-start = (bf16[4,1024]{1,0:T(4,128)(2,1)S(1)}, bf16[4,1024]{1,0:T(4,128)(2,1)S(1)}, u32[]{:S(2)}, u32[]{:S(2)}) collective-permute-start(bf16[4,1024]{1,0:T(4,128)(2,1)S(1)} %get-tuple-element.11), channel_id=1, source_target_pairs={{0,4},{4,8},{8,12},{12,16},{16,20},{20,24},{24,28},{28,0},{1,5},{5... | collective-permute-start | bytes 24584 | tf_op jit(solution)/shard_map/ppermute | solution.py:23
Sparse Core Ops, SparseCore 0:
  9.6 104.6 all-gather.1
  128.3 82.5 reduce-scatter.1
where the time goes:
time: 236 us; the launch traced here: 235 us
  waiting for transfers between devices  143 us (61%)
  matrix products  31 us (13%)
  local copies, waits for them, and re-layouts  19.9 us (8%)
  starting transfers between devices  16.5 us (7%)
  between operations  15.7 us (7%)
  other arithmetic  9.4 us (4%)
    reduce_scatter x1, waiting for transfers between devices, local(): lax.psum_scatter(jnp.dot(own_heads, full_columns, preferred_element_type=...  78.6 us
    all_to_all x1, waiting for transfers between devices, local(): lax.all_to_all(queries.reshape(split_shape), 'fsdp', split_axis=1, concat...  15.8 us
    all_to_all x1, waiting for transfers between devices, local(): lax.all_to_all(keys.reshape(split_shape), 'fsdp', split_axis=1, concat_ax...  14.8 us
    all_to_all x1, waiting for transfers between devices, local(): lax.all_to_all(values.reshape(split_shape), 'fsdp', split_axis=1, concat_...  14.7 us
    dot_general x1, matrix products, local(): jnp.dot(own_heads, full_columns, preferred_element_type=jnp.float32)  13.8 us
    all_gather x1, waiting for transfers between devices, local(): full_columns = lax.all_gather(out_weight, 'win', axis=1, tiled=True)  12.1 us
    dot_general x1, matrix products, softmax_block(): jnp.einsum('hqk,khd->qhd', probability, value_h, preferred_element_type=j...  11.2 us
    unnamed x29, local copies, waits for them, and re-layouts  10.1 us
  transfers between devices with their start and end apart: 7, of which 7 were waited for; matrix products, arithmetic and copies ran while one was open for 15% of the time, Pallas kernels for 0%

commit v1 on v0

v1 whole, which is shorter than its diff:
```python
import functools
import math

import jax
import jax.numpy as jnp
from jax import lax
from jax.experimental import pallas as pl
from jax.experimental.pallas import tpu as pltpu
from jax.sharding import PartitionSpec as P

HEADS = 20
HD = 128
FD = 4
EPSILON = 0.001
MESH = pl.DeviceIdType.MESH
F32 = jnp.float32
BF16 = jnp.bfloat16


def kernel(
    ring, n_blk, q_ref, k_ref, v_ref, stream_ref, ow_ref, gate_ref, shift_ref, scale_ref, wt_ref,
    lat_ref, step_ref, inter_ref, ramps_ref, out_ref,
    qkv, attended, weights, residual, side_out, side_in, own_out, own_in, cross_hold, cross_out,
    cross_in, hidden, flat, fresh, before, after,
    qkv_send, qkv_recv, qkv_local, w_send, w_recv, w_local, res_sem, side_send, side_recv,
    own_send, own_recv, cross_send, cross_recv, edge_send, edge_recv,
):
    win, n_win = lax.axis_index("win"), lax.axis_size("win")
    me, groups = lax.axis_index("fsdp"), lax.axis_size("fsdp")
    rows = q_ref.shape[0]
    heads = qkv.shape[1]
    width = weights.shape[2]
    chip, core = me // 2, me % 2
    sibling = chip * 2 + (1 - core)
    far_chip = 1 - chip
    far = far_chip * 2 + core
    far_sibling = far_chip * 2 + (1 - core)
    inputs = (q_ref, k_ref, v_ref)

    up_win, down_win = lax.rem(win + 1, n_win), lax.rem(win + n_win - 1, n_win)
    half_ring = n_win // 2

    def spot_of(w):
        odd = w % 2
        return (1 - odd) * (w // 2) + odd * (n_win - 1 - w // 2)

    def win_of(spot):
        late = spot // half_ring
        return (1 - late) * (2 * spot) + late * (2 * (n_win - 1 - spot) + 1)

    spot = spot_of(win)
    ring_next = win_of(lax.rem(spot + 1, n_win))
    ring_prev = win_of(lax.rem(spot + n_win - 1, n_win))

    if ring:
        blocks = [win]
        for s in range(1, half_ring):
            blocks.append(win_of(lax.rem(spot - s + n_win, n_win)))
            blocks.append(win_of(lax.rem(spot + s, n_win)))
        blocks.append(win_of(lax.rem(spot + half_ring, n_win)))
    else:
        blocks = [jnp.int32(j) for j in range(n_blk)]

    def columns(j):
        return pl.ds(pl.multiple_of(blocks[j] * width, 128), width)

    def qkv_copy(t, h, to, slot):
        return pltpu.make_async_remote_copy(
            src_ref=inputs[t].at[:, pl.ds(pl.multiple_of((to * heads + h) * HD, HD), HD)],
            dst_ref=qkv.at[t, h, pl.ds(pl.multiple_of(me * rows, rows), rows), :],
            send_sem=qkv_send.at[t, h, slot],
            recv_sem=qkv_recv.at[t, h, me],
            device_id={"fsdp": to},
            device_id_type=MESH,
        )

    def qkv_arrival(t, h, source):
        return pltpu.make_async_remote_copy(
            src_ref=inputs[t].at[:, pl.ds(pl.multiple_of((source * heads + h) * HD, HD), HD)],
            dst_ref=qkv.at[t, h, pl.ds(pl.multiple_of(source * rows, rows), rows), :],
            send_sem=qkv_send.at[t, h, 0],
            recv_sem=qkv_recv.at[t, h, source],
            device_id={"fsdp": source},
            device_id_type=MESH,
        )

    def qkv_own(t, h):
        return pltpu.make_async_copy(
            inputs[t].at[:, pl.ds(pl.multiple_of((me * heads + h) * HD, HD), HD)],
            qkv.at[t, h, pl.ds(pl.multiple_of(me * rows, rows), rows), :],
            qkv_local.at[t, h],
        )

    peers = (far, far_sibling, sibling)

    def weight_copy(src, dst, slot, to):
        return pltpu.make_async_remote_copy(
            src_ref=src, dst_ref=dst, send_sem=w_send.at[slot], recv_sem=w_recv.at[slot],
            device_id={"win": to}, device_id_type=MESH,
        )

    depth_half = weights.shape[1] // 2
    last = n_blk - 1

    def forward_copies(s):
        if s < half_ring:
            up_src = ow_ref if s == 1 else weights.at[2 * s - 3]
            down_src = ow_ref if s == 1 else weights.at[2 * s - 2]
            return (
                weight_copy(up_src, weights.at[2 * s - 1], 2 * s - 2, ring_next),
                weight_copy(down_src, weights.at[2 * s], 2 * s - 1, ring_prev),
            )
        top, low = pl.ds(0, depth_half), pl.ds(depth_half, depth_half)
        return (
            weight_copy(weights.at[2 * s - 3, top], weights.at[last, top], 2 * s - 2, ring_next),
            weight_copy(weights.at[2 * s - 2, low], weights.at[last, low], 2 * s - 1, ring_prev),
        )

    def weight_local(j):
        source = ow_ref if ring else ow_ref.at[:, columns(j)]
        return pltpu.make_async_copy(source, weights.at[j], w_local.at[j])

    def residual_copy(j):
        return pltpu.make_async_copy(
            stream_ref.at[:, columns(j)], residual.at[j], res_sem.at[j]
        )

    barrier = pltpu.get_barrier_semaphore()
    for peer in peers:
        pl.semaphore_signal(barrier, inc=1, device_id={"fsdp": peer}, device_id_type=MESH)
    greeted = [up_win, down_win] + ([ring_next, ring_prev] if ring else [])
    for other in greeted:
        pl.semaphore_signal(barrier, inc=1, device_id={"win": other}, device_id_type=MESH)
    pl.semaphore_wait(barrier, len(peers) + len(greeted))

    def start_heads(kinds):
        def start_head(h, carry):
            for t in kinds:
                for slot, peer in enumerate(peers):
                    qkv_copy(t, h, peer, slot).start()
                qkv_own(t, h).start()
            return carry

        lax.fori_loop(0, heads, start_head, 0)

    start_heads((1, 2))
    if ring:
        for copy in forward_copies(1):
            copy.start()
    start_heads((0,))
    for j in range(1 if ring else n_blk):
        weight_local(j).start()
    for j in range(n_blk):
        residual_copy(j).start()

    factor = math.log2(math.e) / math.sqrt(HD)

    def attend(h, first):
        def piece(i, carry):
            at = pl.ds(pl.multiple_of(first + i * rows, rows), rows)
            query = qkv[0, h, at, :]
            scores = lax.dot_general(
                query, qkv[1, h], (((1,), (1,)), ((), ())), preferred_element_type=F32
            )
            highest = jnp.max(scores, axis=-1, keepdims=True)
            exponent = jnp.exp2((scores - highest) * factor)
            denominator = jnp.sum(exponent, axis=-1, keepdims=True)
            summed = jnp.dot(exponent.astype(BF16), qkv[2, h], preferred_element_type=F32)
            attended[at, pl.ds(pl.multiple_of(h * HD, HD), HD)] = (summed / denominator).astype(
                BF16
            )
            return carry

        lax.fori_loop(0, 2, piece, 0)

    def near_head(h, carry):
        for t in (1, 2):
            for source in peers:
                qkv_arrival(t, h, source).wait_recv()
            qkv_own(t, h).wait()
        qkv_arrival(0, h, sibling).wait_recv()
        qkv_own(0, h).wait()
        attend(h, chip * 2 * rows)
        return carry

    lax.fori_loop(0, heads, near_head, 0)
    if ring:
        for copy in forward_copies(1):
            copy.wait_recv()
        for copy in forward_copies(2):
            copy.start()

    def far_head(h, carry):
        for source in (far, far_sibling):
            qkv_arrival(0, h, source).wait_recv()
        attend(h, far_chip * 2 * rows)
        return carry

    lax.fori_loop(0, heads, far_head, 0)

    def part_copy(src, dst, send, recv, j, to):
        return pltpu.make_async_remote_copy(
            src_ref=src.at[j], dst_ref=dst.at[j], send_sem=send.at[j], recv_sem=recv.at[j],
            device_id={"fsdp": to}, device_id_type=MESH,
        )

    def side_copy(j):
        return part_copy(side_out, side_in, side_send, side_recv, j, sibling)

    def own_copy(j):
        return part_copy(own_out, own_in, own_send, own_recv, j, sibling)

    def cross_copy(j):
        return part_copy(cross_out, cross_in, cross_send, cross_recv, j, far)

    def product(group, j):
        at = pl.ds(pl.multiple_of(group * rows, rows), rows)
        return jnp.dot(attended[at, :], weights[j], preferred_element_type=F32)

    for j in range(n_blk):
        if not ring or j == 0:
            weight_local(j).wait()
        elif j % 2 == 1:
            s = (j + 1) // 2
            if s > 1:
                for copy in forward_copies(s):
                    copy.wait_recv()
                if s < half_ring:
                    for copy in forward_copies(s + 1):
                        copy.start()
        side_out[j] = product(far_sibling, j).astype(BF16)
        side_copy(j).start()
        cross_hold[...] = product(far, j)
        own_out[j] = product(sibling, j).astype(BF16)
        own_copy(j).start()
        hidden[j] = product(me, j)
        side_copy(j).wait_recv()
        cross_out[j] = (cross_hold[...] + side_in[j].astype(F32)).astype(BF16)
        cross_copy(j).start()
        residual_copy(j).wait()
        own_copy(j).wait_recv()
        hidden[j] = residual[j].astype(F32) + gate_ref[:, columns(j)] * (
            hidden[j] + own_in[j].astype(F32)
        )

    centres, spreads = [], []
    for j in range(n_blk):
        cross_copy(j).wait_recv()
        block = hidden[j] + gate_ref[:, columns(j)] * cross_in[j].astype(F32)
        hidden[j] = block
        centre = jnp.sum(block, axis=-1, keepdims=True) * (1.0 / width)
        centred = block - centre
        centres.append(centre)
        spreads.append(jnp.sum(centred * centred, axis=-1, keepdims=True))
    mean = functools.reduce(jnp.add, centres) * (1.0 / n_blk)
    spread = functools.reduce(jnp.add, spreads)
    for centre in centres:
        spread = spread + width * (centre - mean) * (centre - mean)
    inverse = 1.0 / jnp.sqrt(spread * (1.0 / (width * n_blk)) + EPSILON)
    velocity = None
    for j in range(n_blk):
        modulated = (
            (hidden[j] - mean) * inverse * scale_ref[:, columns(j)] + shift_ref[:, columns(j)]
        ).astype(BF16)
        term = lax.dot_general(
            modulated, wt_ref[:, columns(j)], (((1,), (1,)), ((), ())), preferred_element_type=F32
        )
        velocity = term if velocity is None else velocity + term

    channels = wt_ref.shape[0]
    frames, wide = lat_ref.shape
    per_frame = wide // channels
    flat[:, :channels] = velocity
    step = step_ref[0]
    for p in range(0, per_frame, 2):
        pair = jnp.concatenate(
            [flat[pl.ds(p + i, frames, stride=per_frame), :][:, :channels] for i in range(2)],
            axis=1,
        )
        at = pl.ds(p * channels, 2 * channels)
        fresh[:, at] = lat_ref[:, at] + step * pair

    edge = before.shape[0]

    def edge_copy(src, dst, slot, to):
        return pltpu.make_async_remote_copy(
            src_ref=src, dst_ref=dst, send_sem=edge_send.at[slot], recv_sem=edge_recv.at[slot],
            device_id={"win": to}, device_id_type=MESH,
        )

    end_rows = pl.ds(frames - edge, edge)
    edges = (
        edge_copy(fresh.at[end_rows], before, 0, up_win),
        edge_copy(fresh.at[pl.ds(0, edge)], after, 1, down_win),
    )
    for copy in edges:
        copy.start()
    if frames > 2 * edge:
        middle = pl.ds(edge, frames - 2 * edge)
        out_ref[middle, :] = fresh[middle, :]
    index = lax.broadcasted_iota(jnp.int32, (edge, 1), 0)
    over_prev, over_next = inter_ref[down_win], inter_ref[win]
    zero = jnp.zeros((edge, 1), jnp.int32)

    def blend(aligned, mine, theirs_w, mine_w):
        theirs = theirs_w.astype(F32)
        own = jnp.where(mine_w > 0, mine_w, 1).astype(F32)
        return (theirs * aligned + own * mine) / (theirs + own)

    for copy in edges:
        copy.wait_recv()

    weight_theirs, weight_own = zero, zero
    for i in range(FD):
        hit = (index == i) & (index < over_prev)
        weight_theirs = jnp.where(hit, ramps_ref[down_win, 2 * i], weight_theirs)
        weight_own = jnp.where(hit, ramps_ref[down_win, 2 * i + 1], weight_own)
    aligned = jnp.zeros((edge, wide), F32)
    chosen = before[...]
    for o in range(1, FD + 1):
        hit = (zero + over_prev) == o
        aligned = jnp.where(hit, pltpu.roll(chosen, o, 0), aligned)
    out_ref[:edge, :] = blend(aligned, fresh[:edge, :], weight_theirs, weight_own)

    weight_theirs, weight_own = zero, zero
    for i in range(FD):
        hit = (index == edge - over_next + i)
        weight_own = jnp.where(hit, ramps_ref[win, 2 * i], weight_own)
        weight_theirs = jnp.where(hit, ramps_ref[win, 2 * i + 1], weight_theirs)
    aligned = jnp.zeros((edge, wide), F32)
    chosen = after[...]
    for o in range(1, FD + 1):
        hit = (zero + over_next) == o
        aligned = jnp.where(hit, pltpu.roll(chosen, edge - o, 0), aligned)
    out_ref[end_rows, :] = blend(aligned, fresh[end_rows, :], weight_theirs, weight_own)

    def finish_head(h, carry):
        for t in range(3):
            for slot, peer in enumerate(peers):
                qkv_copy(t, h, peer, slot).wait_send()
        return carry

    lax.fori_loop(0, heads, finish_head, 0)
    if ring:
        for s in range(1, half_ring + 1):
            for copy in forward_copies(s):
                copy.wait_send()
    for j in range(n_blk):
        side_copy(j).wait_send()
        own_copy(j).wait_send()
        cross_copy(j).wait_send()
    for copy in edges:
        copy.wait_send()


def local(
    queries,
    keys,
    values,
    stream,
    out_weight,
    gate,
    head_shift,
    head_scale,
    head_weight,
    latents,
    step_size,
    intersections,
    ramps,
):
    rows, features = queries.shape
    groups, n_win = lax.axis_size("fsdp"), lax.axis_size("win")
    heads = features // HD // groups
    depth, part = out_weight.shape
    model = stream.shape[1]
    ring = part % 128 == 0 and n_win % 2 == 0 and n_win >= 6
    if ring:
        n_blk, width = n_win, part
    else:
        n_blk = 8
        width = model // n_blk
        out_weight = lax.all_gather(out_weight, "win", axis=1, tiled=True)
    frames, wide = latents.shape
    edge = 8
    any_spec = pl.BlockSpec(memory_space=pl.ANY)
    vmem = pl.BlockSpec(memory_space=pltpu.VMEM)
    smem = pl.BlockSpec(memory_space=pltpu.SMEM)
    dma = pltpu.SemaphoreType.DMA
    parts = pltpu.VMEM((n_blk, rows, width), BF16)
    return pl.pallas_call(
        functools.partial(kernel, ring, n_blk),
        out_shape=jax.ShapeDtypeStruct(latents.shape, latents.dtype),
        in_specs=[any_spec] * 5 + [vmem] * 5 + [smem] * 3,
        out_specs=vmem,
        scratch_shapes=[
            pltpu.VMEM((3, heads, groups * rows, HD), BF16),
            pltpu.VMEM((groups * rows, heads * HD), BF16),
            pltpu.VMEM((n_blk, depth, width), BF16),
            parts, parts, parts, parts, parts,
            pltpu.VMEM((rows, width), F32),
            parts, parts,
            pltpu.VMEM((n_blk, rows, width), F32),
            pltpu.VMEM((rows, 128), F32),
            pltpu.VMEM((frames, wide), F32),
            pltpu.VMEM((edge, wide), F32),
            pltpu.VMEM((edge, wide), F32),
            dma((3, heads, 3)), dma((3, heads, groups)), dma((3, heads)),
            dma((n_blk,)), dma((n_blk,)), dma((n_blk,)), dma((n_blk,)),
            dma((n_blk,)), dma((n_blk,)), dma((n_blk,)), dma((n_blk,)),
            dma((n_blk,)), dma((n_blk,)), dma((2,)), dma((2,)),
        ],
        compiler_params=pltpu.CompilerParams(
            collective_id=0, has_side_effects=True, vmem_limit_bytes=60 * 1024 * 1024
        ),
    )(
        queries, keys, values, stream, out_weight,
        gate[None, :], head_shift[None, :], head_scale[None, :], head_weight.T, latents,
        step_size, intersections, ramps.reshape(n_win, -1),
    )


def solution(mesh):
    in_specs = (
        P(("win", "fsdp"), None),
        P(("win", "fsdp"), None),
        P(("win", "fsdp"), None),
        P(("win", "fsdp"), None),
        P("fsdp", "win"),
        P(),
        P(),
        P(),
        P(),
        P("win", "fsdp"),
        P(),
        P(),
        P(),
    )
    out_specs = P("win", "fsdp")
    return jax.shard_map(local, mesh=mesh, in_specs=in_specs, out_specs=out_specs, check_vma=False)
```

time: 236 us -> 124 us (0.53)
  waiting for transfers between devices: 143 us -> 0 us
  Pallas kernels: 0 us -> 121 us
  matrix products: 31 us -> 0 us
  local copies, waits for them, and re-layouts: 19.9 us -> 2.82 us
  starting transfers between devices: 16.5 us -> 0 us
  between operations: 15.7 us -> 0.66 us
  other arithmetic: 9.4 us -> 0 us
    pallas_call x0 -> x1, Pallas kernels: none -> 121 us  [local(): pl.pallas_call(functools.partial(kernel, ring, n_blk), out_shape=jax.Shap...]
    reduce_scatter x1 -> x0, waiting for transfers between devices: 78.6 us -> none  [local(): lax.psum_scatter(jnp.dot(own_heads, full_columns, preferred_element_type=...]
    all_to_all x3 -> x0, waiting for transfers between devices: 45.2 us -> none  [the longest x1 15.8 us: local(): lax.all_to_all(queries.reshape(split_shape), 'fsdp', split_axis=1, concat...]
    dot_general x8 -> x0, matrix products: 31 us -> none  [the longest x1 13.8 us: local(): jnp.dot(own_heads, full_columns, preferred_element_type=jnp.float32)]
    all_to_all x3 -> x0, starting transfers between devices: 12.1 us -> none  [the longest x1 4.3 us: local(): lax.all_to_all(values.reshape(split_shape), 'fsdp', split_axis=1, concat_...]
    all_gather x1 -> x0, waiting for transfers between devices: 12.1 us -> none  [local(): full_columns = lax.all_gather(out_weight, 'win', axis=1, tiled=True)]
    reduce_sum x5 -> x0, other arithmetic: 8.69 us -> none  [the longest x1 3.69 us: softmax_block(): denominator = jnp.sum(exponent, axis=-1)]
    unnamed x29 -> x1, local copies, waits for them, and re-layouts: 10.1 us -> 1.47 us
  transfers between devices with their start and end apart: 7 -> 0, of which waited for: 7 -> 0; matrix products, arithmetic and copies ran while one was open for 15% -> 0% of each run, Pallas kernels for 0% -> 0%
where the time goes in v1:
time: 124 us
  Pallas kernels  121 us (98%)
  local copies, waits for them, and re-layouts  2.82 us (2%)
    pallas_call x1, Pallas kernels, local(): pl.pallas_call(functools.partial(kernel, ring, n_blk), out_shape=jax.Shap...  121 us

profile of v1, /device:TPU:0, one launch (start us, length us, event | category | flops | bytes accessed | tf_op | source)
XLA Modules:
  0.0 124.1 jit_solution(2971216963709509097)
XLA Ops:
  0.7 1.3 %copy.14.ramps_ref = s32[8,8]{1,0:T(8,128)} copy(s32[8,8]{0,1:T(8,128)} %bitcast.9) | data formatting | bytes 512 | tf_op jit(solution)/shard_map/reshape | solution.py:418
  2.0 120.6 %shard_map.127 = f32[16,1024]{1,0:T(8,128)} custom-call(bf16[256,2560]{1,0:T(8,128)(2,1)} %q_ref.1, bf16[256,2560]{1,0:T(8,128)(2,1)} %k_ref.1, bf16[256,2560]{1,0:T(8,128)(2,1)} %v_ref.1, bf16[256,5120]{1,0:T(8,128)(2,1)} %stream_ref.1, bf16[640,640]{1,0:T(8,128)(2,1)} %ow_ref.1, f32[1,5120]{1,0:T(1,128)} %bitcast.6, f32[1,5120]{1,0:T(1,128)} %bitcast.7, ...), custom_call_target="tpu_custom_call" | custom-call | tf_op jit(solution)/shard_map/pallas_call | solution.py:390
  122.6 1.5 %copy.17 = f32[16,1024]{1,0:T(8,128)} copy(f32[16,1024]{1,0:T(8,128)} %shard_map.127) | data formatting | bytes 131072

commit v2 on v1

--- a/solution.py
+++ b/solution.py
@@ -21,7 +21,7 @@
     ring, n_blk, q_ref, k_ref, v_ref, stream_ref, ow_ref, gate_ref, shift_ref, scale_ref, wt_ref,
     lat_ref, step_ref, inter_ref, ramps_ref, out_ref,
     qkv, attended, weights, residual, side_out, side_in, own_out, own_in, cross_hold, cross_out,
-    cross_in, hidden, flat, fresh, before, after,
+    cross_in, hidden, flat, fresh, before, after, head_rows,
     qkv_send, qkv_recv, qkv_local, w_send, w_recv, w_local, res_sem, side_send, side_recv,
     own_send, own_recv, cross_send, cross_recv, edge_send, edge_recv,
 ):
@@ -152,6 +152,13 @@
         weight_local(j).start()
     for j in range(n_blk):
         residual_copy(j).start()
+
+    head = wt_ref[...].astype(F32)
+    for i, vector in enumerate((scale_ref, shift_ref)):
+        head_rows[8 * i : 8 * i + 8] = lax.dot_general(
+            jnp.broadcast_to(vector[...], (8, head.shape[1])), head, (((1,), (1,)), ((), ())),
+            precision=lax.Precision.HIGHEST, preferred_element_type=F32,
+        )
 
     factor = math.log2(math.e) / math.sqrt(HD)
 
@@ -243,13 +250,20 @@
             hidden[j] + own_in[j].astype(F32)
         )
 
-    centres, spreads = [], []
+    centres, spreads, raw, pivot = [], [], None, None
     for j in range(n_blk):
         cross_copy(j).wait_recv()
         block = hidden[j] + gate_ref[:, columns(j)] * cross_in[j].astype(F32)
-        hidden[j] = block
-        centre = jnp.sum(block, axis=-1, keepdims=True) * (1.0 / width)
-        centred = block - centre
+        if j == 0:
+            pivot = jnp.sum(block, axis=-1, keepdims=True) * (1.0 / width)
+        shifted = block - pivot
+        term = lax.dot_general(
+            (shifted * scale_ref[:, columns(j)]).astype(BF16), wt_ref[:, columns(j)],
+            (((1,), (1,)), ((), ())), preferred_element_type=F32,
+        )
+        raw = term if raw is None else raw + term
+        centre = jnp.sum(shifted, axis=-1, keepdims=True) * (1.0 / width)
+        centred = shifted - centre
         centres.append(centre)
         spreads.append(jnp.sum(centred * centred, axis=-1, keepdims=True))
     mean = functools.reduce(jnp.add, centres) * (1.0 / n_blk)
@@ -257,15 +271,7 @@
     for centre in centres:
         spread = spread + width * (centre - mean) * (centre - mean)
     inverse = 1.0 / jnp.sqrt(spread * (1.0 / (width * n_blk)) + EPSILON)
-    velocity = None
-    for j in range(n_blk):
-        modulated = (
-            (hidden[j] - mean) * inverse * scale_ref[:, columns(j)] + shift_ref[:, columns(j)]
-        ).astype(BF16)
-        term = lax.dot_general(
-            modulated, wt_ref[:, columns(j)], (((1,), (1,)), ((), ())), preferred_element_type=F32
-        )
-        velocity = term if velocity is None else velocity + term
+    velocity = inverse * (raw - mean * head_rows[:1]) + head_rows[8:9]
 
     channels = wt_ref.shape[0]
     frames, wide = lat_ref.shape
@@ -313,8 +319,8 @@
     weight_theirs, weight_own = zero, zero
     for i in range(FD):
         hit = (index == i) & (index < over_prev)
-        weight_theirs = jnp.where(hit, ramps_ref[down_win, 2 * i], weight_theirs)
-        weight_own = jnp.where(hit, ramps_ref[down_win, 2 * i + 1], weight_own)
+        weight_theirs = jnp.where(hit, ramps_ref[2 * i, down_win], weight_theirs)
+        weight_own = jnp.where(hit, ramps_ref[2 * i + 1, down_win], weight_own)
     aligned = jnp.zeros((edge, wide), F32)
     chosen = before[...]
     for o in range(1, FD + 1):
@@ -325,8 +331,8 @@
     weight_theirs, weight_own = zero, zero
     for i in range(FD):
         hit = (index == edge - over_next + i)
-        weight_own = jnp.where(hit, ramps_ref[win, 2 * i], weight_own)
-        weight_theirs = jnp.where(hit, ramps_ref[win, 2 * i + 1], weight_theirs)
+        weight_own = jnp.where(hit, ramps_ref[2 * i, win], weight_own)
+        weight_theirs = jnp.where(hit, ramps_ref[2 * i + 1, win], weight_theirs)
     aligned = jnp.zeros((edge, wide), F32)
     chosen = after[...]
     for o in range(1, FD + 1):
@@ -404,6 +410,7 @@
             pltpu.VMEM((frames, wide), F32),
             pltpu.VMEM((edge, wide), F32),
             pltpu.VMEM((edge, wide), F32),
+            pltpu.VMEM((16, head_weight.shape[1]), F32),
             dma((3, heads, 3)), dma((3, heads, groups)), dma((3, heads)),
             dma((n_blk,)), dma((n_blk,)), dma((n_blk,)), dma((n_blk,)),
             dma((n_blk,)), dma((n_blk,)), dma((n_blk,)), dma((n_blk,)),
@@ -415,7 +422,7 @@
     )(
         queries, keys, values, stream, out_weight,
         gate[None, :], head_shift[None, :], head_scale[None, :], head_weight.T, latents,
-        step_size, intersections, ramps.reshape(n_win, -1),
+        step_size, intersections, jnp.transpose(ramps, (1, 2, 0)).reshape(-1, n_win),
     )
 
 

time: 124 us -> 122 us (0.984)
  local copies, waits for them, and re-layouts: 2.82 us -> 1.47 us
    reshape x1 -> x0, local copies, waits for them, and re-layouts: 1.35 us -> none  [local(): ramps.reshape(n_win, -1)]
where the time goes in v2:
time: 122 us
  Pallas kernels  120 us (98%)
  local copies, waits for them, and re-layouts  1.47 us (1%)
    pallas_call x1, Pallas kernels, local(): pl.pallas_call(functools.partial(kernel, ring, n_blk), out_shape=jax.Shap...  120 us

profile of v2, /device:TPU:0, one launch (start us, length us, event | category | flops | bytes accessed | tf_op | source)
XLA Modules:
  0.0 121.8 jit_solution(15383120598783172319)
XLA Ops:
  0.7 119.7 %shard_map.127 = f32[16,1024]{1,0:T(8,128)} custom-call(bf16[256,2560]{1,0:T(8,128)(2,1)} %q_ref.1, bf16[256,2560]{1,0:T(8,128)(2,1)} %k_ref.1, bf16[256,2560]{1,0:T(8,128)(2,1)} %v_ref.1, bf16[256,5120]{1,0:T(8,128)(2,1)} %stream_ref.1, bf16[640,640]{1,0:T(8,128)(2,1)} %ow_ref.1, f32[1,5120]{1,0:T(1,128)} %bitcast.8, f32[1,5120]{1,0:T(1,128)} %bitcast.9, ...), custom_call_target="tpu_custom_call" | custom-call | tf_op jit(solution)/shard_map/pallas_call | solution.py:396
  120.4 1.5 %copy.16 = f32[16,1024]{1,0:T(8,128)} copy(f32[16,1024]{1,0:T(8,128)} %shard_map.127) | data formatting | bytes 131072
